TPU v7x, 256 devices: a whole 4x4x8 slice. The times are simulated.
256 devices in a mesh: dp: 32 (over z_hi, y, core), level: 8 (over x, z_lo).
Axes of the slice: x: 4, y: 4, z: 8 (z_hi: 4, z_lo: 2; z = z_hi * 2 + z_lo), core: 2. Of those that a mesh axis runs over, the one named last changes fastest.
Arguments:
- token_ids: int32 [32, 8, 1536], P('dp', 'level'), may hold values from 0 to 1023
- decoded_mask: int32 [32, 8, 1536], P('dp', 'level'), may hold values 0 or 1
- levels_done: int32 [32], P('dp'), may hold values from 0 to 7
- code_tables: bfloat16 [8, 1024, 1024], P('level'), may hold values from -6 to 6
- mask_vectors: bfloat16 [8, 1024], P('level'), may hold values from -6 to 6
- w_qkv: bfloat16 [3, 1024, 1024], P(None, 'dp', 'level'), may hold values from -6 to 6
- w_out: bfloat16 [1024, 1024], P('level', 'dp'), may hold values from -0.1875 to 0.1875
- w_expand: bfloat16 [1024, 2048], P('dp'), may hold values from -0.1875 to 0.1875
- w_depth: bfloat16 [5, 1024], replicated, may hold values from -2.5 to 2.5
- w_project: bfloat16 [1024, 1024], P('dp'), may hold values from -0.1875 to 0.1875
- level_heads: bfloat16 [8, 1024, 1024], P('level'), may hold values from -0.1875 to 0.1875
Outputs:
- logits: bfloat16 [32, 8, 1536, 1024], P('dp', 'level')
Inputs may be any that keep to these rules, and one draw needn't show every extreme that they name: `levels_done`: levels below it are fully decoded; the level equal to it is the one being decoded.
All inputs are finite; a program needn't handle non-finite values. No bound on the sum of `decoded_mask` on one device may be relied on, other than what follows from the above.
Results may differ from a plain program's by a relative error of at most 0.006.
Values may be sent and summed in bfloat16 or wider, within the bound.
A program may use at most 128 MiB of HBM per device.

v0:
```python
import jax
import jax.numpy as jnp
from jax import lax
from jax.sharding import PartitionSpec as P

HEADS = 16


def copy_for_each(x, axis):
    copies = jnp.broadcast_to(x, (lax.axis_size(axis), *x.shape))
    return lax.all_to_all(copies, axis, split_axis=0, concat_axis=0, tiled=True)


def laid_out(tiles, dim):
    tiles = jnp.moveaxis(tiles, 0, dim)
    dims = tiles.shape
    return tiles.reshape(*dims[:dim], dims[dim] * dims[dim + 1], *dims[dim + 2 :])


def gather_directly(x, axis, dim):
    tiles = copy_for_each(x, axis)
    return laid_out(tiles, dim)


def side_by_side(arrays, axis, dim, along):
    ends, at = ([], 0)
    for a in arrays[:-1]:
        at += a.shape[along]
        ends.append(at)
    both = jnp.concatenate(arrays, axis=along)
    return tuple(jnp.split(lax.all_gather(both, axis, axis=dim, tiled=True), ends, axis=along))


def with_halo(x, sides, width):
    for axis, dim in sides:
        devices, length = (lax.axis_size(axis), x.shape[dim])
        up = [(i, (i + 1) % devices) for i in range(devices - 1)]
        down = [(j, i) for i, j in up]
        last = lax.slice_in_dim(x, length - width, length, axis=dim)
        leading = lax.slice_in_dim(x, 0, width, axis=dim)
        before = lax.ppermute(last, axis, up)
        after = lax.ppermute(leading, axis, down)
        x = jnp.concatenate([before, x, after], axis=dim)
    return x


def layer_norm(values):
    centered = values - jnp.mean(values, axis=-1, keepdims=True)
    variance = jnp.mean(centered * centered, axis=-1, keepdims=True)
    return centered * lax.rsqrt(variance + 1e-05)


def contract_with(left, shard_piece):
    return jnp.dot(left, shard_piece, preferred_element_type=jnp.float32)


def contract_three(left, shard_piece):
    return jnp.einsum("fk,jkc->jfc", left, shard_piece, preferred_element_type=jnp.float32)


def body(
    token_ids,
    decoded_mask,
    levels_done,
    code_tables,
    mask_vectors,
    w_qkv,
    w_out,
    w_expand,
    w_depth,
    w_project,
    level_heads,
):
    frames = token_ids.shape[2]
    model_width = code_tables.shape[2]
    groups = lax.axis_size("level")
    level_index = lax.axis_index("level")
    local_rows = frames // groups
    head_dim = model_width // HEADS
    scale = head_dim ** (-0.5)
    id_row = token_ids[0, 0]
    flag_row = decoded_mask[0, 0]
    done_count = levels_done[0]
    own_table = code_tables[0]
    fill_row = mask_vectors[0].astype(jnp.float32)
    all_live = level_index < done_count
    current = level_index == done_count
    use_token = all_live | current & (flag_row == 1)
    codes = lax.broadcasted_iota(jnp.int32, (frames, own_table.shape[0]), 1)
    onehot = (id_row[:, None] == codes).astype(jnp.bfloat16)
    picked = jnp.dot(onehot, own_table, preferred_element_type=jnp.float32)
    level_terms = (
        jnp.where(use_token[:, None], picked, fill_row[None, :])
        .astype(jnp.bfloat16)
        .reshape(groups, local_rows, model_width)
    )
    received = lax.all_to_all(level_terms, "level", split_axis=0, concat_axis=0, tiled=True)
    own_rows = jnp.sum(received, axis=0, dtype=jnp.float32)
    normed = layer_norm(own_rows).astype(jnp.bfloat16)
    full_columns = gather_directly(w_qkv, "level", 2)
    projected = contract_three(
        normed, lax.all_gather(full_columns, "dp", axis=1, tiled=True)
    ).astype(jnp.bfloat16)
    queries = projected[0].reshape(local_rows, HEADS, head_dim)
    running_max = jnp.full((HEADS, local_rows), -1e30, jnp.float32)
    accumulated = jnp.zeros((local_rows, HEADS, head_dim), jnp.float32)
    key_piece, value_piece = side_by_side((projected[1], projected[2]), "level", 0, 1)
    piece_rows = key_piece.shape[0]
    key_three = key_piece.reshape(piece_rows, HEADS, head_dim)
    value_three = value_piece.reshape(piece_rows, HEADS, head_dim)
    scores = (
        jnp.einsum("qhd,khd->hqk", queries, key_three, preferred_element_type=jnp.float32) * scale
    )
    new_max = jnp.maximum(running_max, jnp.max(scores, axis=-1))
    shrink = jnp.exp(running_max - new_max)
    weights = jnp.exp(scores - new_max[:, :, None])
    weight_sum = jnp.sum(weights, axis=-1)
    added = jnp.einsum(
        "hqk,khd->qhd",
        weights.astype(jnp.bfloat16),
        value_three,
        preferred_element_type=jnp.float32,
    )
    accumulated = accumulated * shrink.T[:, :, None] + added
    running_max, weight_sum, accumulated = (new_max, weight_sum, accumulated)
    attended = (
        (accumulated / weight_sum.T[:, :, None])
        .reshape(local_rows, model_width)
        .astype(jnp.bfloat16)
    )
    out_full = gather_directly(w_out, "level", 0)
    after_attn = own_rows + jnp.dot(
        attended,
        lax.all_gather(out_full, "dp", axis=1, tiled=True),
        preferred_element_type=jnp.float32,
    )
    normed_two = layer_norm(after_attn).astype(jnp.bfloat16)
    gate_linear = contract_with(normed_two, lax.all_gather(w_expand, "dp", axis=0, tiled=True))
    gated = (gate_linear[:, :model_width] * jax.nn.sigmoid(gate_linear[:, model_width:])).astype(
        jnp.bfloat16
    )
    half_width = w_depth.shape[0] // 2
    padded = with_halo(gated, (("level", 0),), half_width)
    conv = jnp.zeros((local_rows, model_width), jnp.float32)
    for tap_index in range(w_depth.shape[0]):
        conv = conv + padded[tap_index : tap_index + local_rows].astype(jnp.float32) * w_depth[
            tap_index
        ].astype(jnp.float32)
    activated = (conv * jax.nn.sigmoid(conv)).astype(jnp.bfloat16)
    after_conv = after_attn + contract_with(
        activated, lax.all_gather(w_project, "dp", axis=0, tiled=True)
    )
    final_norm = layer_norm(after_conv).astype(jnp.bfloat16)
    own_head = level_heads[0]
    logits = jnp.dot(
        lax.all_gather(final_norm, "level", axis=0, tiled=True),
        own_head,
        preferred_element_type=jnp.float32,
    ).astype(jnp.bfloat16)
    return logits[None, None]


def solution(mesh):
    return jax.shard_map(
        body,
        mesh=mesh,
        in_specs=(
            P("dp", "level", None),
            P("dp", "level", None),
            P("dp"),
            P("level", None, None),
            P("level", None),
            P(None, "dp", "level"),
            P("level", "dp"),
            P("dp", None),
            P(),
            P("dp", None),
            P("level", None, None),
        ),
        out_specs=P("dp", "level", None, None),
        check_vma=False,
    )
```

profile of v0, /device:TPU:1, one launch (start us, length us, event | category | flops | bytes accessed | tf_op | source)
XLA Modules:
  0.0 501.6 jit_solution(8657905231968769645)
XLA Ops:
  7.5 11.9 %all_to_all.15 = bf16[8,3,32,128]{3,2,1,0:T(8,128)(2,1)S(1)} all-to-all(bf16[8,3,32,128]{3,2,1,0:T(8,128)(2,1)S(1)} %broadcast_in_dim.57), channel_id=1, replica_groups=mesh['dp'=32,'level'=8] {'level'}, dimensions={0} | all-to-all | bytes 393216 | tf_op jit(solution)/shard_map/all_to_all | solution.py:11
  22.9 4.3 select_convert_fusion
  27.2 60.7 %all_to_all.16 = bf16[8,192,1024]{2,1,0:T(8,128)(2,1)S(1)} all-to-all(bf16[8,192,1024]{2,1,0:T(8,128)(2,1)S(1)} %bitcast.63), channel_id=1, replica_groups=mesh['dp'=32,'level'=8] {'level'}, dimensions={0} | all-to-all | bytes 6291456 | tf_op jit(solution)/shard_map/all_to_all | solution.py:97
  87.9 1.8 convert_reduce_fusion
  90.0 13.5 %all-gather.7.cloned.1.call-done = bf16[3,1024,1024]{2,1,0:T(8,128)(2,1)} async-done(((bf16[3,32,1024]{2,1,0:T(8,128)(2,1)}), bf16[3,1024,1024]{2,1,0:T(8,128)(2,1)}) %all-gather.7.cloned.1.call-update) | async-done | bytes 6291472 | tf_op jit(solution)/shard_map/all_gather | solution.py:102
  103.5 4.2 fusion.11
  108.8 9.0 %all_to_all.17 = bf16[8,128,32]{1,2,0:T(8,128)(2,1)S(1)} all-to-all(bf16[8,128,32]{1,2,0:T(8,128)(2,1)S(1)} %broadcast_in_dim.59), channel_id=1, replica_groups=mesh['dp'=32,'level'=8] {'level'}, dimensions={0} | all-to-all | bytes 131072 | tf_op jit(solution)/shard_map/all_to_all | solution.py:11
  119.9 119.0 %all-gather.9.cloned.1.call-done = bf16[1536,2048]{1,0:T(8,128)(2,1)} async-done(((bf16[192,2048]{1,0:T(8,128)(2,1)}), bf16[1536,2048]{1,0:T(8,128)(2,1)}) %all-gather.9.cloned.1.call-update) | async-done | bytes 6291472 | tf_op jit(solution)/shard_map/all_gather | solution.py:31
  238.9 6.3 %fusion.45 = (bf16[1536,1024]{1,0:T(8,128)(2,1)}, bf16[1536,1024]{1,0:T(8,128)(2,1)}) fusion(bf16[1536,2048]{1,0:T(8,128)(2,1)} %all-gather.9.cloned.1.call-done), kind=kLoop, calls=%fused_computation.81 | loop fusion | bytes 12582912 | tf_op jit(solution)/shard_map/split | solution.py:31
  245.2 4.7 copy.27
  249.9 4.7 copy.26
  254.6 11.1 %multiply_reduce_fusion = (f32[16,192]{1,0:T(8,128)S(1)}, f32[16,192,1536]{2,1,0:T(8,128)}) fusion(bf16[192,16,64]{0,2,1:T(8,128)(2,1)S(1)} %bitcast.61, bf16[1536,16,64]{0,2,1:T(8,128)(2,1)} %bitcast.60), kind=kOutput, calls=%fused_computation.1 | convolution fusion | flops 613413888 | bytes 22425600 | tf_op jit(solution)/shard_map/qhd,khd->hqk/dot_general | solution.py:112
  265.7 9.6 %fusion = f32[16,192]{1,0:T(8,128)S(1)} fusion(f32[16,192,1536]{2,1,0:T(8,128)} %get-tuple-element.22, f32[16,192]{1,0:T(8,128)S(1)} %get-tuple-element.20), kind=kLoop, calls=%fused_computation.2 | loop fusion | flops 14152704 | bytes 18898944 | tf_op jit(solution)/shard_map/reduce_sum | solution.py:117
  275.3 11.1 %divide_convert_fusion = bf16[192,16,64]{0,2,1:T(8,128)(2,1)S(1)} fusion(bf16[1536,16,64]{0,2,1:T(8,128)(2,1)} %bitcast.62, f32[16,192,1536]{2,1,0:T(8,128)} %get-tuple-element.22, f32[16,192]{1,0:T(8,128)S(1)} %get-tuple-element.20, f32[192,16]{0,1:T(8,128)S(1)} %bitcast.65, f32[192,16]{0,1:T(8,128)S(1)} %get-tuple-element.19), kind=kOutput, calls=%fused_computation.23 | convolution fusion | flops 618725376 | bytes 22450176 | tf_op jit(solution)/shard_map/hqk,khd->qhd/dot_general | solution.py:118
  286.4 11.3 %all-gather.11.cloned.1.call-done = bf16[1024,1024]{0,1:T(8,128)(2,1)} async-done(((bf16[1024,32]{0,1:T(8,128)(2,1)}), bf16[1024,1024]{0,1:T(8,128)(2,1)}) %all-gather.11.cloned.1.call-update) | async-done | bytes 2097168 | tf_op jit(solution)/shard_map/all_gather | solution.py:134
  297.7 2.5 fusion.48
  300.5 57.0 %all-gather.13.cloned.1.call-done = bf16[1024,2048]{1,0:T(8,128)(2,1)} async-done(((bf16[32,2048]{1,0:T(8,128)(2,1)}), bf16[1024,2048]{1,0:T(8,128)(2,1)}) %all-gather.13.cloned.1.call-update) | async-done | bytes 4194320 | tf_op jit(solution)/shard_map/all_gather | solution.py:138
  357.5 3.2 fusion.29
  360.9 1.3 collective-permute-start.1
  362.2 4.2 collective-permute-start
  366.5 46.3 %all-gather.15.cloned.1.call-done = bf16[1024,1024]{1,0:T(8,128)(2,1)} async-done(((bf16[32,1024]{1,0:T(8,128)(2,1)}), bf16[1024,1024]{1,0:T(8,128)(2,1)}) %all-gather.15.cloned.1.call-update) | async-done | bytes 2097168 | tf_op jit(solution)/shard_map/all_gather | solution.py:151
  412.8 2.7 fusion.49
  416.7 70.3 %all-gather.17.cloned.1.call-done = bf16[1536,1024]{1,0:T(8,128)(2,1)} async-done(((bf16[192,1024]{1,0:T(8,128)(2,1)}), bf16[1536,1024]{1,0:T(8,128)(2,1)}) %all-gather.17.cloned.1.call-update) | async-done | bytes 3145744 | tf_op jit(solution)/shard_map/all_gather | solution.py:156
  487.0 7.8 %fusion.7 = bf16[1,1,1536,1024]{3,2,1,0:T(8,128)(2,1)} fusion(bf16[1536,1024]{1,0:T(8,128)(2,1)} %all-gather.17.cloned.1.call-done, bf16[1,1024,1024]{2,1,0:T(8,128)(2,1)} %param.21), kind=kOutput, calls=%fused_computation.13 | convolution fusion | flops 3222798336 | bytes 8388608 | tf_op jit(solution)/shard_map/dot_general | solution.py:155
  (46 shorter events, 8.9 us)
Async XLA Ops:
  6.5 16.4 %copy-start = (bf16[1,1024,1024]{2,1,0:T(8,128)(2,1)S(1)}, bf16[1,1024,1024]{2,1,0:T(8,128)(2,1)}, u32[]{:S(2)}) copy-start(bf16[1,1024,1024]{2,1,0:T(8,128)(2,1)} %param.14) | copy-start | bytes 6291460
  6.5 96.9 %all-gather.7.cloned.1.call-start = ((), (), s32[]{:S(2)}) async-start(), calls=%async_computation.3 | async-start | bytes 6488064 | tf_op jit(solution)/shard_map/all_gather | solution.py:102
  20.1 218.8 %all-gather.9.cloned.1.call-start = ((), (), s32[]{:S(2)}) async-start(), calls=%async_computation.4 | async-start | bytes 7077888 | tf_op jit(solution)/shard_map/all_gather | solution.py:31
  107.7 1.1 copy-start.3
  108.8 189.0 %all-gather.11.cloned.1.call-start = ((), (), s32[]{:S(2)}) async-start(), calls=%async_computation.5 | async-start | bytes 2162688 | tf_op jit(solution)/shard_map/all_gather | solution.py:134
  118.5 239.0 %all-gather.13.cloned.1.call-start = ((), (), s32[]{:S(2)}) async-start(), calls=%async_computation.6 | async-start | bytes 4325376 | tf_op jit(solution)/shard_map/all_gather | solution.py:138
  119.1 293.7 %all-gather.15.cloned.1.call-start = ((), (), s32[]{:S(2)}) async-start(), calls=%async_computation.7 | async-start | bytes 2162688 | tf_op jit(solution)/shard_map/all_gather | solution.py:151
  119.6 367.3 %all-gather.17.cloned.1.call-start = ((), (), s32[]{:S(2)}) async-start(), calls=%async_computation.8 | async-start | bytes 3538944 | tf_op jit(solution)/shard_map/all_gather | solution.py:156
  300.5 66.0 %copy-start.2 = (bf16[5,1024]{1,0:T(8,128)(2,1)S(1)}, bf16[5,1024]{1,0:T(8,128)(2,1)}, u32[]{:S(2)}) copy-start(bf16[5,1024]{1,0:T(8,128)(2,1)} %param.19) | copy-start | bytes 30724
  360.9 51.8 %collective-permute-start.1 = (bf16[2,1024]{1,0:T(2,128)(2,1)S(1)}, bf16[2,1024]{1,0:T(2,128)(2,1)S(1)}, u32[]{:S(2)}, u32[]{:S(2)}) collective-permute-start(bf16[2,1024]{1,0:T(2,128)(2,1)S(1)} %get-tuple-element.13), channel_id=1, source_target_pairs={{1,0},{2,1},{3,2},{4,3},{5,4},{6,5},{7,6},{9,8},{10,9},{11,10},{12... | collective-permute-start | bytes 12296 | tf_op jit(solution)/shard_map/ppermute | solution.py:42
  362.2 50.5 %collective-permute-start = (bf16[2,1024]{1,0:T(2,128)(2,1)S(1)}, bf16[2,1024]{1,0:T(2,128)(2,1)S(1)}, u32[]{:S(2)}, u32[]{:S(2)}) collective-permute-start(bf16[2,1024]{1,0:T(2,128)(2,1)S(1)} %get-tuple-element.12), channel_id=1, source_target_pairs={{0,1},{1,2},{2,3},{3,4},{4,5},{5,6},{6,7},{8,9},{9,10},{10,11},{11... | collective-permute-start | bytes 12296 | tf_op jit(solution)/shard_map/ppermute | solution.py:41
  487.0 7.8 %copy-start.1 = (bf16[1,1024,1024]{2,1,0:T(8,128)(2,1)S(1)}, bf16[1,1024,1024]{2,1,0:T(8,128)(2,1)}, u32[]{:S(2)}) copy-start(bf16[1,1024,1024]{2,1,0:T(8,128)(2,1)} %param.14) | copy-start | bytes 6291460
Sparse Core Ops, SparseCore 0:
  20.2 83.2 all-gather.6
  108.9 129.9 all-gather.8
  241.5 56.1 all-gather.10
  300.1 57.3 all-gather.12
  359.9 52.8 all-gather.14
  416.8 70.1 all-gather.16
where the time goes:
time: 502 us
  waiting for transfers between devices  318 us (63%)
  blocking collectives  81.6 us (16%)
  matrix products  46.9 us (9%)
  local copies, waits for them, and re-layouts  18.2 us (4%)
  other arithmetic  16.4 us (3%)
  between operations  14.3 us (3%)
  starting transfers between devices  5.7 us (1%)
    all_gather x1, waiting for transfers between devices, side_by_side(): lax.all_gather(both, axis, axis=dim, tiled=True)  119 us
    all_gather x1, waiting for transfers between devices, body(): lax.all_gather(final_norm, 'level', axis=0, tiled=True)  70.3 us
    all_to_all x1, blocking collectives, body(): lax.all_to_all(level_terms, 'level', split_axis=0, concat_axis=0, tiled=T...  60.7 us
    all_gather x1, waiting for transfers between devices, body(): lax.all_gather(w_expand, 'dp', axis=0, tiled=True)  57 us
    all_gather x1, waiting for transfers between devices, body(): lax.all_gather(w_project, 'dp', axis=0, tiled=True)  46.3 us
    all_to_all x2, blocking collectives, copy_for_each(): return lax.all_to_all(copies, axis, split_axis=0, concat_axis=0, tiled=True)  20.9 us
    split x3, local copies, waits for them, and re-layouts, side_by_side(): jnp.split(lax.all_gather(both, axis, axis=dim, tiled=True), ends, axis=al...  15.7 us
    all_gather x1, waiting for transfers between devices, body(): lax.all_gather(full_columns, 'dp', axis=1, tiled=True)  13.5 us
  transfers between devices with their start and end apart: 8, of which 6 were waited for; matrix products, arithmetic and copies ran while one was open for 13% of the time, Pallas kernels for 0%

commit v1 on v0

--- a/solution.py
+++ b/solution.py
@@ -148,7 +148,10 @@
         ].astype(jnp.float32)
     activated = (conv * jax.nn.sigmoid(conv)).astype(jnp.bfloat16)
     after_conv = after_attn + contract_with(
-        activated, lax.all_gather(w_project, "dp", axis=0, tiled=True)
+        activated,
+        jnp.concatenate(
+            lax.all_to_all(jnp.stack([w_project] * lax.axis_size("dp")), "dp", 0, 0), axis=0
+        ),
     )
     final_norm = layer_norm(after_conv).astype(jnp.bfloat16)
     own_head = level_heads[0]

time: 502 us -> 505 us (level)
  starting transfers between devices: 5.7 us -> 14.8 us
  waiting for transfers between devices: 318 us -> 311 us
    all_gather x1 -> x0, waiting for transfers between devices: 46.3 us -> none  [body(): lax.all_gather(w_project, 'dp', axis=0, tiled=True)]
    all_gather x1, waiting for transfers between devices: 119 us -> 154 us  [side_by_side(): lax.all_gather(both, axis, axis=dim, tiled=True)]
    all_to_all x0 -> x1, starting transfers between devices: none -> 9.16 us  [body(): lax.all_to_all(jnp.stack([w_project] * lax.axis_size('dp')), 'dp', 0, 0)]
where the time goes in v1:
time: 505 us; the launch traced here: 504 us
  waiting for transfers between devices  311 us (62%)
  blocking collectives  81.6 us (16%)
  matrix products  46.9 us (9%)
  local copies, waits for them, and re-layouts  19.8 us (4%)
  other arithmetic  16.4 us (3%)
  starting transfers between devices  14.8 us (3%)
  between operations  14 us (3%)
    all_gather x1, waiting for transfers between devices, side_by_side(): lax.all_gather(both, axis, axis=dim, tiled=True)  154 us
    all_gather x1, waiting for transfers between devices, body(): lax.all_gather(final_norm, 'level', axis=0, tiled=True)  73.9 us
    all_to_all x1, blocking collectives, body(): lax.all_to_all(level_terms, 'level', split_axis=0, concat_axis=0, tiled=T...  60.7 us
    all_gather x1, waiting for transfers between devices, body(): lax.all_gather(w_expand, 'dp', axis=0, tiled=True)  57 us
    all_to_all x2, blocking collectives, copy_for_each(): return lax.all_to_all(copies, axis, split_axis=0, concat_axis=0, tiled=True)  20.9 us
    split x3, local copies, waits for them, and re-layouts, side_by_side(): jnp.split(lax.all_gather(both, axis, axis=dim, tiled=True), ends, axis=al...  15.7 us
    all_gather x1, waiting for transfers between devices, body(): lax.all_gather(full_columns, 'dp', axis=1, tiled=True)  13.5 us
    all_gather x1, waiting for transfers between devices, body(): lax.all_gather(out_full, 'dp', axis=1, tiled=True)  11.4 us
  transfers between devices with their start and end apart: 8, of which 6 were waited for; matrix products, arithmetic and copies ran while one was open for 13% of the time, Pallas kernels for 0%

profile of v1, /device:TPU:1, one launch (start us, length us, event | category | flops | bytes accessed | tf_op | source)
XLA Modules:
  0.0 504.1 jit_solution(9351163729252406555)
XLA Ops:
  7.5 11.9 %all_to_all.20 = bf16[8,3,32,128]{3,2,1,0:T(8,128)(2,1)S(1)} all-to-all(bf16[8,3,32,128]{3,2,1,0:T(8,128)(2,1)S(1)} %broadcast_in_dim.57), channel_id=1, replica_groups=mesh['dp'=32,'level'=8] {'level'}, dimensions={0} | all-to-all | bytes 393216 | tf_op jit(solution)/shard_map/all_to_all | solution.py:11
  22.9 4.3 select_convert_fusion
  27.2 60.7 %all_to_all.21 = bf16[8,192,1024]{2,1,0:T(8,128)(2,1)S(1)} all-to-all(bf16[8,192,1024]{2,1,0:T(8,128)(2,1)S(1)} %bitcast.64), channel_id=1, replica_groups=mesh['dp'=32,'level'=8] {'level'}, dimensions={0} | all-to-all | bytes 6291456 | tf_op jit(solution)/shard_map/all_to_all | solution.py:97
  87.9 1.8 convert_reduce_fusion
  90.0 13.5 %all-gather.6.cloned.1.call-done = bf16[3,1024,1024]{2,1,0:T(8,128)(2,1)} async-done(((bf16[3,32,1024]{2,1,0:T(8,128)(2,1)}), bf16[3,1024,1024]{2,1,0:T(8,128)(2,1)}) %all-gather.6.cloned.1.call-update) | async-done | bytes 6291472 | tf_op jit(solution)/shard_map/all_gather | solution.py:102
  103.5 4.2 fusion.11
  108.9 9.0 %all_to_all.22 = bf16[8,128,32]{1,2,0:T(8,128)(2,1)S(1)} all-to-all(bf16[8,128,32]{1,2,0:T(8,128)(2,1)S(1)} %broadcast_in_dim.59), channel_id=1, replica_groups=mesh['dp'=32,'level'=8] {'level'}, dimensions={0} | all-to-all | bytes 131072 | tf_op jit(solution)/shard_map/all_to_all | solution.py:11
  119.1 1.6 stack.2
  120.6 9.2 %all-to-all-start.3 = ((bf16[32,32,1024]{2,1,0:T(8,128)(2,1)}), bf16[32,32,1024]{2,1,0:T(8,128)(2,1)}, u32[]{:S(2)}, u32[]{:S(2)}) async-start(bf16[32,32,1024]{2,1,0:T(8,128)(2,1)} %stack.2), calls=%async_computation.3 | async-start | bytes 4194304 | tf_op jit(solution)/shard_map/all_to_all | solution.py:153
  130.1 153.8 %all-gather.8.cloned.1.call-done = bf16[1536,2048]{1,0:T(8,128)(2,1)} async-done(((bf16[192,2048]{1,0:T(8,128)(2,1)}), bf16[1536,2048]{1,0:T(8,128)(2,1)}) %all-gather.8.cloned.1.call-update) | async-done | bytes 6291472 | tf_op jit(solution)/shard_map/all_gather | solution.py:31
  283.9 6.3 %fusion.45 = (bf16[1536,1024]{1,0:T(8,128)(2,1)}, bf16[1536,1024]{1,0:T(8,128)(2,1)}) fusion(bf16[1536,2048]{1,0:T(8,128)(2,1)} %all-gather.8.cloned.1.call-done), kind=kLoop, calls=%fused_computation.81 | loop fusion | bytes 12582912 | tf_op jit(solution)/shard_map/split | solution.py:31
  290.2 4.7 copy.27
  294.9 4.7 copy.26
  299.6 11.1 %multiply_reduce_fusion = (f32[16,192]{1,0:T(8,128)S(1)}, f32[16,192,1536]{2,1,0:T(8,128)}) fusion(bf16[192,16,64]{0,2,1:T(8,128)(2,1)S(1)} %bitcast.62, bf16[1536,16,64]{0,2,1:T(8,128)(2,1)} %bitcast.61), kind=kOutput, calls=%fused_computation.1 | convolution fusion | flops 613413888 | bytes 22425600 | tf_op jit(solution)/shard_map/qhd,khd->hqk/dot_general | solution.py:112
  310.6 9.6 %fusion = f32[16,192]{1,0:T(8,128)S(1)} fusion(f32[16,192,1536]{2,1,0:T(8,128)} %get-tuple-element.22, f32[16,192]{1,0:T(8,128)S(1)} %get-tuple-element.20), kind=kLoop, calls=%fused_computation.2 | loop fusion | flops 14152704 | bytes 18898944 | tf_op jit(solution)/shard_map/reduce_sum | solution.py:117
  320.2 11.1 %divide_convert_fusion = bf16[192,16,64]{0,2,1:T(8,128)(2,1)S(1)} fusion(bf16[1536,16,64]{0,2,1:T(8,128)(2,1)} %bitcast.63, f32[16,192,1536]{2,1,0:T(8,128)} %get-tuple-element.22, f32[16,192]{1,0:T(8,128)S(1)} %get-tuple-element.20, f32[192,16]{0,1:T(8,128)S(1)} %bitcast.66, f32[192,16]{0,1:T(8,128)S(1)} %get-tuple-element.19), kind=kOutput, calls=%fused_computation.23 | convolution fusion | flops 618725376 | bytes 22450176 | tf_op jit(solution)/shard_map/hqk,khd->qhd/dot_general | solution.py:118
  331.3 11.4 %all-gather.10.cloned.1.call-done = bf16[1024,1024]{0,1:T(8,128)(2,1)} async-done(((bf16[1024,32]{0,1:T(8,128)(2,1)}), bf16[1024,1024]{0,1:T(8,128)(2,1)}) %all-gather.10.cloned.1.call-update) | async-done | bytes 2097168 | tf_op jit(solution)/shard_map/all_gather | solution.py:134
  342.7 2.5 fusion.48
  345.5 57.0 %all-gather.12.cloned.1.call-done = bf16[1024,2048]{1,0:T(8,128)(2,1)} async-done(((bf16[32,2048]{1,0:T(8,128)(2,1)}), bf16[1024,2048]{1,0:T(8,128)(2,1)}) %all-gather.12.cloned.1.call-update) | async-done | bytes 4194320 | tf_op jit(solution)/shard_map/all_gather | solution.py:138
  402.4 3.2 fusion.29
  407.2 4.2 collective-permute-start
  411.9 2.7 fusion.49
  415.8 73.9 %all-gather.14.cloned.1.call-done = bf16[1536,1024]{1,0:T(8,128)(2,1)} async-done(((bf16[192,1024]{1,0:T(8,128)(2,1)}), bf16[1536,1024]{1,0:T(8,128)(2,1)}) %all-gather.14.cloned.1.call-update) | async-done | bytes 3145744 | tf_op jit(solution)/shard_map/all_gather | solution.py:159
  489.8 7.8 %fusion.7 = bf16[1,1,1536,1024]{3,2,1,0:T(8,128)(2,1)} fusion(bf16[1536,1024]{1,0:T(8,128)(2,1)} %all-gather.14.cloned.1.call-done, bf16[1,1024,1024]{2,1,0:T(8,128)(2,1)} %param.21), kind=kOutput, calls=%fused_computation.13 | convolution fusion | flops 3222798336 | bytes 8388608 | tf_op jit(solution)/shard_map/dot_general | solution.py:158
  (48 shorter events, 10.0 us)
Async XLA Ops:
  6.5 16.4 %copy-start = (bf16[1,1024,1024]{2,1,0:T(8,128)(2,1)S(1)}, bf16[1,1024,1024]{2,1,0:T(8,128)(2,1)}, u32[]{:S(2)}) copy-start(bf16[1,1024,1024]{2,1,0:T(8,128)(2,1)} %param.14) | copy-start | bytes 6291460
  6.5 96.9 %all-gather.6.cloned.1.call-start = ((), (), s32[]{:S(2)}) async-start(), calls=%async_computation.4 | async-start | bytes 6488064 | tf_op jit(solution)/shard_map/all_gather | solution.py:102
  20.1 263.8 %all-gather.8.cloned.1.call-start = ((), (), s32[]{:S(2)}) async-start(), calls=%async_computation.5 | async-start | bytes 7077888 | tf_op jit(solution)/shard_map/all_gather | solution.py:31
  107.7 1.1 copy-start.4
  107.7 11.4 %copy-start.2 = (bf16[32,1024]{1,0:T(8,128)(2,1)S(1)}, bf16[32,1024]{1,0:T(8,128)(2,1)}, u32[]{:S(2)}) copy-start(bf16[32,1024]{1,0:T(8,128)(2,1)} %param.20) | copy-start | bytes 196612
  108.8 233.9 %all-gather.10.cloned.1.call-start = ((), (), s32[]{:S(2)}) async-start(), calls=%async_computation.6 | async-start | bytes 2162688 | tf_op jit(solution)/shard_map/all_gather | solution.py:134
  118.5 283.9 %all-gather.12.cloned.1.call-start = ((), (), s32[]{:S(2)}) async-start(), calls=%async_computation.7 | async-start | bytes 4325376 | tf_op jit(solution)/shard_map/all_gather | solution.py:138
  120.6 290.8 %all-to-all-start.3 = ((bf16[32,32,1024]{2,1,0:T(8,128)(2,1)}), bf16[32,32,1024]{2,1,0:T(8,128)(2,1)}, u32[]{:S(2)}, u32[]{:S(2)}) async-start(bf16[32,32,1024]{2,1,0:T(8,128)(2,1)} %stack.2), calls=%async_computation.3 | async-start | bytes 4194304 | tf_op jit(solution)/shard_map/all_to_all | solution.py:153
  129.8 360.0 %all-gather.14.cloned.1.call-start = ((), (), s32[]{:S(2)}) async-start(), calls=%async_computation.8 | async-start | bytes 3538944 | tf_op jit(solution)/shard_map/all_gather | solution.py:159
  345.5 66.0 %copy-start.3 = (bf16[5,1024]{1,0:T(8,128)(2,1)S(1)}, bf16[5,1024]{1,0:T(8,128)(2,1)}, u32[]{:S(2)}) copy-start(bf16[5,1024]{1,0:T(8,128)(2,1)} %param.19) | copy-start | bytes 30724
  405.9 5.6 %collective-permute-start.1 = (bf16[2,1024]{1,0:T(2,128)(2,1)S(1)}, bf16[2,1024]{1,0:T(2,128)(2,1)S(1)}, u32[]{:S(2)}, u32[]{:S(2)}) collective-permute-start(bf16[2,1024]{1,0:T(2,128)(2,1)S(1)} %get-tuple-element.13), channel_id=1, source_target_pairs={{1,0},{2,1},{3,2},{4,3},{5,4},{6,5},{7,6},{9,8},{10,9},{11,10},{12... | collective-permute-start | bytes 12296 | tf_op jit(solution)/shard_map/ppermute | solution.py:42
  407.2 4.7 collective-permute-start
  489.8 7.8 %copy-start.1 = (bf16[1,1024,1024]{2,1,0:T(8,128)(2,1)S(1)}, bf16[1,1024,1024]{2,1,0:T(8,128)(2,1)}, u32[]{:S(2)}) copy-start(bf16[1,1024,1024]{2,1,0:T(8,128)(2,1)} %param.14) | copy-start | bytes 6291460
Sparse Core Ops, SparseCore 0:
  20.2 83.2 all-gather.5
  108.9 174.9 all-gather.7
  286.4 56.2 all-gather.9
  345.1 57.2 all-gather.11
  416.0 73.7 all-gather.13
